TPU v7x, 32 devices: a whole 2x2x4 slice. The times are simulated.
32 devices in a mesh: site: 2 (over x), row: 4 (over z), col: 4 (over y, core).
Axes of the slice: x: 2, y: 2, z: 4, core: 2. Of those that a mesh axis runs over, the one named last changes fastest.
Arguments:
- pair_array: bfloat16 [128, 64, 128], P(('site', 'row'), 'col'), parts along dimension 0, may hold values from -6 to 6
- in_gain: float32 [128], replicated, may hold values from 0.25 to 1.75
- left_weight: bfloat16 [256, 128], P('site'), parts along dimension 0, may hold values from -0.5 to 0.5
- right_weight: bfloat16 [256, 128], P('site'), parts along dimension 0, may hold values from -0.5 to 0.5
- mid_gain: float32 [128], replicated, may hold values from 0.25 to 1.75
- out_weight: bfloat16 [256, 128], P('site'), parts along dimension 0, may hold values from -0.5 to 0.5
- out_gate: bfloat16 [256, 128], P('site'), parts along dimension 0, may hold values from -0.5 to 0.5
Outputs:
- triangle_out: bfloat16 [128, 64, 128], P(('site', 'row'), 'col'), parts along dimension 0
There are 2 independent parts, one for each index of `site`. A program takes and returns all parts, laid end to end along the dimension named above; an argument that names none is the same for every part. Nothing has to cross between parts.
All inputs are finite; a program needn't handle non-finite values.
Results may differ from a plain program's by a relative error of at most 0.012.
Values may be sent and summed in bfloat16 or wider, within the bound.
A program may use at most 64 MiB of HBM per device.

v0:
```python
import jax
import jax.numpy as jnp
from jax import lax
from jax.sharding import PartitionSpec as P


def norm_channels(values, channel_gain):
    centred = values - jnp.mean(values, axis=-1, keepdims=True)
    return (
        centred
        * lax.rsqrt(jnp.mean(centred * centred, axis=-1, keepdims=True) + 1e-05)
        * channel_gain
    )


def both_factors(pair_in, in_gain, left_weight, right_weight):
    ready = norm_channels(pair_in.astype(jnp.float32), in_gain).astype(jnp.bfloat16)
    ready = lax.optimization_barrier(ready)
    left = jnp.einsum("ijc,cd->ijd", ready, left_weight, preferred_element_type=jnp.float32)
    right = jnp.einsum("ijc,cd->ijd", ready, right_weight, preferred_element_type=jnp.float32)
    return (ready, left.astype(jnp.bfloat16), right.astype(jnp.bfloat16))


def finish_pair(mixed, ready, mid_gain, out_weight, out_gate):
    scaled = norm_channels(mixed.astype(jnp.float32), mid_gain).astype(jnp.bfloat16)
    scaled = lax.optimization_barrier(scaled)
    gate = jax.nn.sigmoid(
        jnp.einsum("ijc,cd->ijd", ready, out_gate, preferred_element_type=jnp.float32)
    )
    return (
        jnp.einsum("ijd,dc->ijc", scaled, out_weight, preferred_element_type=jnp.float32) * gate
    ).astype(jnp.bfloat16)


def body(pair_array, in_gain, left_weight, right_weight, mid_gain, out_weight, out_gate):
    ready, left, right = both_factors(pair_array, in_gain, left_weight, right_weight)
    count = pair_array.shape[0] * lax.axis_size("row")
    left_lines, right_lines = (
        lax.all_to_all(left, "row", split_axis=2, concat_axis=0, tiled=True),
        lax.all_to_all(right, "row", split_axis=2, concat_axis=0, tiled=True),
    )
    strip = jnp.einsum(
        "kid,kjd->ijd",
        lax.all_gather(left_lines, "col", axis=1, tiled=True),
        right_lines,
        preferred_element_type=jnp.float32,
    )
    strip = (strip * count ** (-0.5)).astype(jnp.bfloat16)
    mixed = lax.all_to_all(strip, "row", split_axis=0, concat_axis=2, tiled=True)
    return finish_pair(mixed, ready, mid_gain, out_weight, out_gate)


def solution(mesh):
    return jax.shard_map(
        body,
        mesh=mesh,
        in_specs=(
            P(("site", "row"), "col", None),
            P(),
            P("site", None),
            P("site", None),
            P(),
            P("site", None),
            P("site", None),
        ),
        out_specs=P(("site", "row"), "col", None),
        check_vma=False,
    )
```

profile of v0, /device:TPU:0, one launch (start us, length us, event | category | flops | bytes accessed | tf_op | source)
XLA Modules:
  0.0 46.4 jit_solution(6474242782185736790)
XLA Ops:
  0.0 0.0 copy-start
  0.0 0.0 copy-start.1
  0.0 1.0 %convert_reduce_fusion = f32[16,16]{1,0:T(8,128)S(1)} fusion(bf16[16,16,128]{2,1,0:T(8,128)(2,1)} %param.7), kind=kLoop, calls=%fused_computation.15 | loop fusion | flops 65280 | bytes 66560 | tf_op jit(solution)/shard_map/reduce_sum | solution.py:8
  1.0 0.0 copy-done.1
  1.0 0.2 fusion.10
  1.2 0.0 copy-start.4
  1.3 0.6 %copy-done.4 = f32[128]{0:T(128)S(1)} copy-done((f32[128]{0:T(128)S(1)}, f32[128]{0:T(128)}, u32[]{:S(2)}) %copy-start.4) | copy-done | bytes 536
  1.9 0.1 fusion.12
  2.0 0.0 copy-done
  2.0 0.1 convolution_convert_fusion.1
  2.2 0.4 copy.32
  2.6 1.2 %reshape.39 = bf16[4,2,4096]{2,1,0:T(2,128)(2,1)} reshape(bf16[128,16,16]{2,1,0:T(8,128)(2,1)S(1)} %bitcast.43) | data formatting | bytes 131072
  3.8 0.0 copy-start.2
  3.8 6.5 %all-to-all-start = ((bf16[4,2,4096]{2,1,0:T(2,128)(2,1)}), bf16[4,2,4096]{2,1,0:T(2,128)(2,1)S(1)}, u32[]{:S(2)}, u32[]{:S(2)}) async-start(bf16[4,2,4096]{2,1,0:T(2,128)(2,1)} %reshape.39), calls=%async_computation | async-start | bytes 131072 | tf_op jit(solution)/shard_map/all_to_all | solution.py:40
  10.3 0.0 copy-done.2
  10.3 0.1 convolution_convert_fusion
  10.4 0.4 copy.34
  10.9 1.2 %reshape.41 = bf16[4,2,4096]{2,1,0:T(2,128)(2,1)} reshape(bf16[128,16,16]{2,1,0:T(8,128)(2,1)S(1)} %bitcast.44) | data formatting | bytes 131072
  12.0 4.0 %all-to-all-done = bf16[4,2,4096]{2,1,0:T(2,128)(2,1)S(1)} async-done(((bf16[4,2,4096]{2,1,0:T(2,128)(2,1)}), bf16[4,2,4096]{2,1,0:T(2,128)(2,1)S(1)}, u32[]{:S(2)}, u32[]{:S(2)}) %all-to-all-start) | async-done | bytes 65568 | tf_op jit(solution)/shard_map/all_to_all | solution.py:40
  16.0 3.3 %all-to-all-start.1 = ((bf16[4,2,4096]{2,1,0:T(2,128)(2,1)}), bf16[4,2,4096]{2,1,0:T(2,128)(2,1)S(1)}, u32[]{:S(2)}, u32[]{:S(2)}) async-start(bf16[4,2,4096]{2,1,0:T(2,128)(2,1)} %reshape.41), calls=%async_computation.1 | async-start | bytes 131072 | tf_op jit(solution)/shard_map/all_to_all | solution.py:39
  19.3 0.4 reshape.40
  19.7 0.4 copy.33
  20.2 0.3 copy.37
  20.5 4.6 %all-to-all-done.1 = bf16[4,2,4096]{2,1,0:T(2,128)(2,1)S(1)} async-done(((bf16[4,2,4096]{2,1,0:T(2,128)(2,1)}), bf16[4,2,4096]{2,1,0:T(2,128)(2,1)S(1)}, u32[]{:S(2)}, u32[]{:S(2)}) %all-to-all-start.1) | async-done | bytes 65568 | tf_op jit(solution)/shard_map/all_to_all | solution.py:39
  25.0 0.4 reshape.42
  25.4 0.4 copy.35
  25.9 0.3 copy.36
  26.2 7.2 %all_gather.3 = bf16[64,64,32]{0,1,2:T(8,128)(2,1)S(1)} all-gather(bf16[64,16,32]{0,1,2:T(8,128)(2,1)S(1)} %copy.36), channel_id=1, replica_groups=mesh['site'=2,'row'=4,'col'=4] {'col'}, dimensions={1}, use_global_device_ids=true | all-gather | bytes 327680 | tf_op jit(solution)/shard_map/all_gather | solution.py:44
  33.4 0.4 fusion.1
  33.8 0.3 copy.38
  34.1 0.3 reshape.43
  34.4 8.1 %all_to_all.45 = bf16[4,2,4096]{2,1,0:T(2,128)(2,1)S(1)} all-to-all(bf16[4,2,4096]{2,1,0:T(2,128)(2,1)S(1)} %reshape.43), channel_id=1, replica_groups=mesh['site'=2,'row'=4,'col'=4] {'row'}, dimensions={0} | all-to-all | bytes 131072 | tf_op jit(solution)/shard_map/all_to_all | solution.py:49
  42.5 0.2 reshape.44
  42.7 0.1 fusion.7
  42.8 0.2 multiply_reduce_fusion
  43.1 0.3 copy.39
  43.4 0.0 copy-start.5
  43.5 0.3 reshape.32
  43.7 0.4 copy-done.5
  44.1 0.0 copy-start.3
  44.1 0.1 multiply_convert_fusion
  44.2 0.6 %copy-done.3 = bf16[128,128]{1,0:T(8,128)(2,1)S(1)} copy-done((bf16[128,128]{1,0:T(8,128)(2,1)S(1)}, bf16[128,128]{1,0:T(8,128)(2,1)}, u32[]{:S(2)}) %copy-start.3) | copy-done | bytes 32792
  44.9 0.0 copy-start.6
  44.9 0.1 fusion.14
  45.0 0.6 %copy-done.6 = bf16[128,128]{1,0:T(8,128)(2,1)S(1)} copy-done((bf16[128,128]{1,0:T(8,128)(2,1)S(1)}, bf16[128,128]{1,0:T(8,128)(2,1)}, u32[]{:S(2)}) %copy-start.6) | copy-done | bytes 32792
  45.6 0.8 %fusion.6 = bf16[16,16,128]{2,1,0:T(8,128)(2,1)} fusion(f32[16,16,128]{2,1,0:T(8,128)S(1)} %fusion.14, bf16[16,16,128]{2,1,0:T(8,128)(2,1)S(1)} %fusion.12, bf16[128,128]{1,0:T(8,128)(2,1)S(1)} %copy-done.6), kind=kOutput, calls=%fused_computation.8 | convolution fusion | flops 8552448 | bytes 294912 | tf_op jit(solution)/shard_map/ijc,cd->ijd/dot_general | solution.py:28
  (5 shorter events, 0.1 us)
Async XLA Ops:
  0.0 2.0 %copy-start = (bf16[128,128]{1,0:T(8,128)(2,1)S(1)}, bf16[128,128]{1,0:T(8,128)(2,1)}, u32[]{:S(2)}) copy-start(bf16[128,128]{1,0:T(8,128)(2,1)} %param.10) | copy-start | bytes 98308
  0.0 1.0 %copy-start.1 = (bf16[16,16,128]{2,1,0:T(8,128)(2,1)S(1)}, bf16[16,16,128]{2,1,0:T(8,128)(2,1)}, u32[]{:S(2)}) copy-start(bf16[16,16,128]{2,1,0:T(8,128)(2,1)} %param.7) | copy-start | bytes 196612
  1.2 0.7 %copy-start.4 = (f32[128]{0:T(128)S(1)}, f32[128]{0:T(128)}, u32[]{:S(2)}) copy-start(f32[128]{0:T(128)} %param.8) | copy-start | bytes 1540
  3.8 6.5 %copy-start.2 = (bf16[128,128]{1,0:T(8,128)(2,1)S(1)}, bf16[128,128]{1,0:T(8,128)(2,1)}, u32[]{:S(2)}) copy-start(bf16[128,128]{1,0:T(8,128)(2,1)} %param.9) | copy-start | bytes 98308
  3.8 12.2 %all-to-all-start = ((bf16[4,2,4096]{2,1,0:T(2,128)(2,1)}), bf16[4,2,4096]{2,1,0:T(2,128)(2,1)S(1)}, u32[]{:S(2)}, u32[]{:S(2)}) async-start(bf16[4,2,4096]{2,1,0:T(2,128)(2,1)} %reshape.39), calls=%async_computation | async-start | bytes 131072 | tf_op jit(solution)/shard_map/all_to_all | solution.py:40
  16.0 9.0 %all-to-all-start.1 = ((bf16[4,2,4096]{2,1,0:T(2,128)(2,1)}), bf16[4,2,4096]{2,1,0:T(2,128)(2,1)S(1)}, u32[]{:S(2)}, u32[]{:S(2)}) async-start(bf16[4,2,4096]{2,1,0:T(2,128)(2,1)} %reshape.41), calls=%async_computation.1 | async-start | bytes 131072 | tf_op jit(solution)/shard_map/all_to_all | solution.py:39
  43.4 0.7 %copy-start.5 = (f32[128]{0:T(128)S(1)}, f32[128]{0:T(128)}, u32[]{:S(2)}) copy-start(f32[128]{0:T(128)} %param.11) | copy-start | bytes 1540
  44.1 0.8 %copy-start.3 = (bf16[128,128]{1,0:T(8,128)(2,1)S(1)}, bf16[128,128]{1,0:T(8,128)(2,1)}, u32[]{:S(2)}) copy-start(bf16[128,128]{1,0:T(8,128)(2,1)} %param.12) | copy-start | bytes 98308
  44.9 0.8 %copy-start.6 = (bf16[128,128]{1,0:T(8,128)(2,1)S(1)}, bf16[128,128]{1,0:T(8,128)(2,1)}, u32[]{:S(2)}) copy-start(bf16[128,128]{1,0:T(8,128)(2,1)} %param.13) | copy-start | bytes 98308
where the time goes:
time: 47 us; the launch traced here: 46.4 us
  blocking collectives  15.3 us (33%)
  starting transfers between devices  9.76 us (21%)
  local copies, waits for them, and re-layouts  9.11 us (19%)
  waiting for transfers between devices  8.55 us (18%)
  other arithmetic  1.87 us (4%)
  matrix products  1.61 us (3%)
    all_to_all x1, blocking collectives, body(): lax.all_to_all(strip, 'row', split_axis=0, concat_axis=2, tiled=True)  8.11 us
    all_gather x1, blocking collectives, body(): lax.all_gather(left_lines, 'col', axis=1, tiled=True)  7.2 us
    all_to_all x1, starting transfers between devices, body(): lax.all_to_all(right, 'row', split_axis=2, concat_axis=0, tiled=True)  6.48 us
    unnamed x20, local copies, waits for them, and re-layouts  5.82 us
    all_to_all x1, waiting for transfers between devices, body(): lax.all_to_all(left, 'row', split_axis=2, concat_axis=0, tiled=True)  4.56 us
    all_to_all x1, waiting for transfers between devices, body(): lax.all_to_all(right, 'row', split_axis=2, concat_axis=0, tiled=True)  3.99 us
    all_to_all x1, starting transfers between devices, body(): lax.all_to_all(left, 'row', split_axis=2, concat_axis=0, tiled=True)  3.28 us
    reduce_sum x2, other arithmetic, norm_channels(): centred = values - jnp.mean(values, axis=-1, keepdims=True)  1.14 us
  transfers between devices with their start and end apart: 2, of which 2 were waited for; matrix products, arithmetic and copies ran while one was open for 6% of the time, Pallas kernels for 0%

commit v1 on v0

--- a/solution.py
+++ b/solution.py
@@ -2,6 +2,17 @@
 import jax.numpy as jnp
 from jax import lax
 from jax.sharding import PartitionSpec as P
+from jax.lax import all_to_all, axis_size
+
+apply_lanes_by_axis = lambda vals, mesh_ax: jnp.concatenate(
+    all_to_all(
+        jnp.stack([vals for _ in range(axis_size(mesh_ax))], 0),
+        axis_name=mesh_ax,
+        split_axis=0,
+        concat_axis=0,
+    ),
+    1,
+)
 
 
 def norm_channels(values, channel_gain):
@@ -41,7 +52,7 @@
     )
     strip = jnp.einsum(
         "kid,kjd->ijd",
-        lax.all_gather(left_lines, "col", axis=1, tiled=True),
+        apply_lanes_by_axis(left_lines, "col"),
         right_lines,
         preferred_element_type=jnp.float32,
     )

time: 47 us -> 48.5 us (1.032)
  blocking collectives: 15.3 us -> 8.11 us
  waiting for transfers between devices: 8.55 us -> 12.2 us
  starting transfers between devices: 9.76 us -> 13.2 us
  local copies, waits for them, and re-layouts: 9.11 us -> 10.6 us
    all_gather x1 -> x0, blocking collectives: 7.2 us -> none  [body(): lax.all_gather(left_lines, 'col', axis=1, tiled=True)]
    all_to_all x0 -> x1, waiting for transfers between devices: none -> 4.82 us  [all_to_all(jnp.stack([vals for _ in range(axis_size(mesh_ax))], 0), axis_...]
    all_to_all x0 -> x1, starting transfers between devices: none -> 3.4 us  [all_to_all(jnp.stack([vals for _ in range(axis_size(mesh_ax))], 0), axis_...]
    all_to_all x1, starting transfers between devices: 3.28 us -> 6.48 us  [body(): lax.all_to_all(left, 'row', split_axis=2, concat_axis=0, tiled=True)]
    all_to_all x1, starting transfers between devices: 6.48 us -> 3.29 us  [body(): lax.all_to_all(right, 'row', split_axis=2, concat_axis=0, tiled=True)]
    unnamed x20 -> x23, local copies, waits for them, and re-layouts: 5.82 us -> 7.32 us
    all_to_all x1, waiting for transfers between devices: 4.56 us -> 3.99 us  [body(): lax.all_to_all(left, 'row', split_axis=2, concat_axis=0, tiled=True)]
    all_to_all x1, waiting for transfers between devices: 3.99 us -> 3.44 us  [body(): lax.all_to_all(right, 'row', split_axis=2, concat_axis=0, tiled=True)]
  transfers between devices with their start and end apart: 2 -> 3, of which waited for: 2 -> 3; matrix products, arithmetic and copies ran while one was open for 6% -> 11% of each run, Pallas kernels for 0% -> 0%
where the time goes in v1:
time: 48.5 us; the launch traced here: 47.8 us
  starting transfers between devices  13.2 us (27%)
  waiting for transfers between devices  12.2 us (25%)
  local copies, waits for them, and re-layouts  10.6 us (22%)
  blocking collectives  8.11 us (17%)
  other arithmetic  1.87 us (4%)
  matrix products  1.61 us (3%)
    all_to_all x1, blocking collectives, body(): lax.all_to_all(strip, 'row', split_axis=0, concat_axis=2, tiled=True)  8.11 us
    unnamed x23, local copies, waits for them, and re-layouts  7.32 us
    all_to_all x1, starting transfers between devices, body(): lax.all_to_all(left, 'row', split_axis=2, concat_axis=0, tiled=True)  6.48 us
    all_to_all x1, waiting for transfers between devices, all_to_all(jnp.stack([vals for _ in range(axis_size(mesh_ax))], 0), axis_...  4.82 us
    all_to_all x1, waiting for transfers between devices, body(): lax.all_to_all(left, 'row', split_axis=2, concat_axis=0, tiled=True)  3.99 us
    all_to_all x1, waiting for transfers between devices, body(): lax.all_to_all(right, 'row', split_axis=2, concat_axis=0, tiled=True)  3.44 us
    all_to_all x1, starting transfers between devices, all_to_all(jnp.stack([vals for _ in range(axis_size(mesh_ax))], 0), axis_...  3.4 us
    all_to_all x1, starting transfers between devices, body(): lax.all_to_all(right, 'row', split_axis=2, concat_axis=0, tiled=True)  3.29 us
  transfers between devices with their start and end apart: 3, of which 3 were waited for; matrix products, arithmetic and copies ran while one was open for 11% of the time, Pallas kernels for 0%

profile of v1, /device:TPU:0, one launch (start us, length us, event | category | flops | bytes accessed | tf_op | source)
XLA Modules:
  0.0 47.8 jit_solution(10338723388784889439)
XLA Ops:
  0.0 0.0 copy-start
  0.0 0.0 copy-start.1
  0.0 1.0 %convert_reduce_fusion = f32[16,16]{1,0:T(8,128)S(1)} fusion(bf16[16,16,128]{2,1,0:T(8,128)(2,1)} %param.7), kind=kLoop, calls=%fused_computation.16 | loop fusion | flops 65280 | bytes 66560 | tf_op jit(solution)/shard_map/reduce_sum | solution.py:19
  1.0 0.0 copy-done.1
  1.0 0.2 fusion.11
  1.2 0.0 copy-start.4
  1.3 0.6 %copy-done.4 = f32[128]{0:T(128)S(1)} copy-done((f32[128]{0:T(128)S(1)}, f32[128]{0:T(128)}, u32[]{:S(2)}) %copy-start.4) | copy-done | bytes 536
  1.9 0.1 fusion.13
  2.0 0.0 copy-done
  2.0 0.1 convolution_convert_fusion
  2.2 0.4 copy.36
  2.6 1.2 %reshape.52 = bf16[4,2,4096]{2,1,0:T(2,128)(2,1)} reshape(bf16[128,16,16]{2,1,0:T(8,128)(2,1)S(1)} %bitcast.49) | data formatting | bytes 131072
  3.8 0.0 copy-start.2
  3.8 6.5 %all-to-all-start.1 = ((bf16[4,2,4096]{2,1,0:T(2,128)(2,1)}), bf16[4,2,4096]{2,1,0:T(2,128)(2,1)S(1)}, u32[]{:S(2)}, u32[]{:S(2)}) async-start(bf16[4,2,4096]{2,1,0:T(2,128)(2,1)} %reshape.52), calls=%async_computation.1 | async-start | bytes 131072 | tf_op jit(solution)/shard_map/all_to_all | solution.py:50
  10.3 0.0 copy-done.2
  10.3 0.1 convolution_convert_fusion.1
  10.4 0.4 copy.34
  10.9 1.2 %reshape.50 = bf16[4,2,4096]{2,1,0:T(2,128)(2,1)} reshape(bf16[128,16,16]{2,1,0:T(8,128)(2,1)S(1)} %bitcast.50) | data formatting | bytes 131072
  12.0 4.0 %all-to-all-done.1 = bf16[4,2,4096]{2,1,0:T(2,128)(2,1)S(1)} async-done(((bf16[4,2,4096]{2,1,0:T(2,128)(2,1)}), bf16[4,2,4096]{2,1,0:T(2,128)(2,1)S(1)}, u32[]{:S(2)}, u32[]{:S(2)}) %all-to-all-start.1) | async-done | bytes 65568 | tf_op jit(solution)/shard_map/all_to_all | solution.py:50
  16.0 3.3 %all-to-all-start = ((bf16[4,2,4096]{2,1,0:T(2,128)(2,1)}), bf16[4,2,4096]{2,1,0:T(2,128)(2,1)S(1)}, u32[]{:S(2)}, u32[]{:S(2)}) async-start(bf16[4,2,4096]{2,1,0:T(2,128)(2,1)} %reshape.50), calls=%async_computation | async-start | bytes 131072 | tf_op jit(solution)/shard_map/all_to_all | solution.py:51
  19.3 0.4 reshape.53
  19.7 0.4 copy.37
  20.1 0.3 copy.38
  20.4 0.1 broadcast_bitcast_fusion
  20.5 1.1 %reshape.54 = bf16[4,2,16384]{2,1,0:T(2,128)(2,1)} reshape(bf16[4,16,32,64]{3,2,1,0:T(8,128)(2,1)S(1)} %broadcast_bitcast_fusion) | data formatting | bytes 524288
  21.6 3.4 %all-to-all-done = bf16[4,2,4096]{2,1,0:T(2,128)(2,1)S(1)} async-done(((bf16[4,2,4096]{2,1,0:T(2,128)(2,1)}), bf16[4,2,4096]{2,1,0:T(2,128)(2,1)S(1)}, u32[]{:S(2)}, u32[]{:S(2)}) %all-to-all-start) | async-done | bytes 65568 | tf_op jit(solution)/shard_map/all_to_all | solution.py:51
  25.0 3.4 %all-to-all-start.2 = ((bf16[4,2,16384]{2,1,0:T(2,128)(2,1)}), bf16[4,2,16384]{2,1,0:T(2,128)(2,1)S(1)}, u32[]{:S(2)}, u32[]{:S(2)}) async-start(bf16[4,2,16384]{2,1,0:T(2,128)(2,1)} %reshape.54), calls=%async_computation.2 | async-start | bytes 524288 | tf_op jit(solution)/shard_map/all_to_all | solution.py:8
  28.4 0.4 reshape.51
  28.8 0.4 copy.35
  29.3 0.3 copy.39
  29.6 4.8 %all-to-all-done.2 = bf16[4,2,16384]{2,1,0:T(2,128)(2,1)S(1)} async-done(((bf16[4,2,16384]{2,1,0:T(2,128)(2,1)}), bf16[4,2,16384]{2,1,0:T(2,128)(2,1)S(1)}, u32[]{:S(2)}, u32[]{:S(2)}) %all-to-all-start.2) | async-done | bytes 262176 | tf_op jit(solution)/shard_map/all_to_all | solution.py:8
  34.4 0.3 reshape.55
  34.8 0.4 fusion.1
  35.1 0.3 copy.41
  35.4 0.3 reshape.56
  35.7 8.1 %all_to_all.47 = bf16[4,2,4096]{2,1,0:T(2,128)(2,1)S(1)} all-to-all(bf16[4,2,4096]{2,1,0:T(2,128)(2,1)S(1)} %reshape.56), channel_id=1, replica_groups=mesh['site'=2,'row'=4,'col'=4] {'row'}, dimensions={0} | all-to-all | bytes 131072 | tf_op jit(solution)/shard_map/all_to_all | solution.py:60
  43.8 0.2 reshape.57
  44.1 0.1 fusion.8
  44.2 0.2 multiply_reduce_fusion
  44.5 0.3 copy.42
  44.8 0.0 copy-start.5
  44.8 0.3 reshape.43
  45.1 0.4 copy-done.5
  45.5 0.1 multiply_convert_fusion
  45.6 0.6 %copy-done.3 = bf16[128,128]{1,0:T(8,128)(2,1)S(1)} copy-done((bf16[128,128]{1,0:T(8,128)(2,1)S(1)}, bf16[128,128]{1,0:T(8,128)(2,1)}, u32[]{:S(2)}) %copy-start.3) | copy-done | bytes 32792
  46.2 0.1 fusion.15
  46.4 0.6 %copy-done.6 = bf16[128,128]{1,0:T(8,128)(2,1)S(1)} copy-done((bf16[128,128]{1,0:T(8,128)(2,1)S(1)}, bf16[128,128]{1,0:T(8,128)(2,1)}, u32[]{:S(2)}) %copy-start.6) | copy-done | bytes 32792
  47.0 0.8 %fusion.6 = bf16[16,16,128]{2,1,0:T(8,128)(2,1)} fusion(f32[16,16,128]{2,1,0:T(8,128)S(1)} %fusion.15, bf16[16,16,128]{2,1,0:T(8,128)(2,1)S(1)} %fusion.13, bf16[128,128]{1,0:T(8,128)(2,1)S(1)} %copy-done.6), kind=kOutput, calls=%fused_computation.8 | convolution fusion | flops 8552448 | bytes 294912 | tf_op jit(solution)/shard_map/ijc,cd->ijd/dot_general | solution.py:39
  (7 shorter events, 0.1 us)
Async XLA Ops:
  0.0 2.0 %copy-start = (bf16[128,128]{1,0:T(8,128)(2,1)S(1)}, bf16[128,128]{1,0:T(8,128)(2,1)}, u32[]{:S(2)}) copy-start(bf16[128,128]{1,0:T(8,128)(2,1)} %param.9) | copy-start | bytes 98308
  0.0 1.0 %copy-start.1 = (bf16[16,16,128]{2,1,0:T(8,128)(2,1)S(1)}, bf16[16,16,128]{2,1,0:T(8,128)(2,1)}, u32[]{:S(2)}) copy-start(bf16[16,16,128]{2,1,0:T(8,128)(2,1)} %param.7) | copy-start | bytes 196612
  1.2 0.7 %copy-start.4 = (f32[128]{0:T(128)S(1)}, f32[128]{0:T(128)}, u32[]{:S(2)}) copy-start(f32[128]{0:T(128)} %param.8) | copy-start | bytes 1540
  3.8 6.5 %copy-start.2 = (bf16[128,128]{1,0:T(8,128)(2,1)S(1)}, bf16[128,128]{1,0:T(8,128)(2,1)}, u32[]{:S(2)}) copy-start(bf16[128,128]{1,0:T(8,128)(2,1)} %param.10) | copy-start | bytes 98308
  3.8 12.2 %all-to-all-start.1 = ((bf16[4,2,4096]{2,1,0:T(2,128)(2,1)}), bf16[4,2,4096]{2,1,0:T(2,128)(2,1)S(1)}, u32[]{:S(2)}, u32[]{:S(2)}) async-start(bf16[4,2,4096]{2,1,0:T(2,128)(2,1)} %reshape.52), calls=%async_computation.1 | async-start | bytes 131072 | tf_op jit(solution)/shard_map/all_to_all | solution.py:50
  16.0 9.0 %all-to-all-start = ((bf16[4,2,4096]{2,1,0:T(2,128)(2,1)}), bf16[4,2,4096]{2,1,0:T(2,128)(2,1)S(1)}, u32[]{:S(2)}, u32[]{:S(2)}) async-start(bf16[4,2,4096]{2,1,0:T(2,128)(2,1)} %reshape.50), calls=%async_computation | async-start | bytes 131072 | tf_op jit(solution)/shard_map/all_to_all | solution.py:51
  25.0 9.4 %all-to-all-start.2 = ((bf16[4,2,16384]{2,1,0:T(2,128)(2,1)}), bf16[4,2,16384]{2,1,0:T(2,128)(2,1)S(1)}, u32[]{:S(2)}, u32[]{:S(2)}) async-start(bf16[4,2,16384]{2,1,0:T(2,128)(2,1)} %reshape.54), calls=%async_computation.2 | async-start | bytes 524288 | tf_op jit(solution)/shard_map/all_to_all | solution.py:8
  44.8 0.7 %copy-start.5 = (f32[128]{0:T(128)S(1)}, f32[128]{0:T(128)}, u32[]{:S(2)}) copy-start(f32[128]{0:T(128)} %param.11) | copy-start | bytes 1540
  45.5 0.8 %copy-start.3 = (bf16[128,128]{1,0:T(8,128)(2,1)S(1)}, bf16[128,128]{1,0:T(8,128)(2,1)}, u32[]{:S(2)}) copy-start(bf16[128,128]{1,0:T(8,128)(2,1)} %param.12) | copy-start | bytes 98308
  46.2 0.8 %copy-start.6 = (bf16[128,128]{1,0:T(8,128)(2,1)S(1)}, bf16[128,128]{1,0:T(8,128)(2,1)}, u32[]{:S(2)}) copy-start(bf16[128,128]{1,0:T(8,128)(2,1)} %param.13) | copy-start | bytes 98308
